TPU v7x, 32 devices: a whole 2x2x4 slice. The times are simulated.
32 devices in a mesh: prow: 8 (over z, y), pcol: 4 (over x, core).
Axes of the slice: x: 2, y: 2, z: 4, core: 2. Of those that a mesh axis runs over, the one named last changes fastest.
Arguments:
- iface_tiles: int32 [32, 16], replicated, may hold values from 0 to 63, as said below
- interior_sizes: int32 [32], P(('prow', 'pcol')), may hold values from 128 to 512
- coupling: float32 [32, 512, 2048], P(('prow', 'pcol')), may hold values from -0.25 to 0.25
- factor_inverse: float32 [32, 512, 512], P(('prow', 'pcol')), as said below
- interface_block: float32 [8, 8, 4, 16, 128, 128], P('prow', None, 'pcol'), as said below
Outputs:
- schur: float32 [8, 8, 4, 16, 128, 128], P('prow', None, 'pcol')
- panel: float32 [8, 8, 128, 128], P('prow', None, 'pcol')
Inputs may be any that keep to these rules, and one draw needn't show every extreme that they name: `iface_tiles`: each row holds 16 distinct tile numbers; for every r, exactly 2 of them are r modulo 8; every tile number stands in exactly 8 rows. `factor_inverse`: each matrix is lower triangular with a diagonal between 0.25 and 1. `interface_block`: diagonal entries lie between 80 and 160; other entries are of order one.
All inputs are finite; a program needn't handle non-finite values.
Results may differ from a plain program's by a relative error of at most 0.0001.
Values sent between devices are 32-bit elements; how exact they have to be, the bound alone decides.
A program may use at most 128 MiB of HBM per device.

v0:
```python
import jax
import jax.numpy as jnp
from jax import lax
from jax.sharding import PartitionSpec as P


def broadcast(block, axis, owner):
    block = jnp.where(lax.axis_index(axis) == owner, block, jnp.zeros_like(block))
    return lax.psum(block, axis)


def solve_panel(diag_block, column):
    lower = jnp.linalg.cholesky(0.5 * (diag_block + diag_block.T))
    flat = column.reshape(-1, diag_block.shape[0])
    solved = jax.scipy.linalg.solve_triangular(lower, flat.T, lower=True)
    return solved.T.reshape(column.shape)


def shards(iface_tiles, interior_sizes, coupling, factor_inverse, interface_block):
    rows_grid = lax.axis_size("prow")
    cols_grid = lax.axis_size("pcol")
    prow_index = lax.axis_index("prow")
    pcol_index = lax.axis_index("pcol")
    self_index = prow_index * cols_grid + pcol_index
    domains = iface_tiles.shape[0]
    tile_count = iface_tiles.shape[1]
    tile_width = interface_block.shape[-1]
    local_rows = interface_block.shape[1]
    local_cols = interface_block.shape[3]
    rows_per = tile_count // rows_grid
    cols_per = tile_count // cols_grid
    share_rows = tile_width // cols_grid
    live_count = interior_sizes[0]
    own_coupling = coupling[0]
    own_factor = factor_inverse[0]
    interior = own_coupling.shape[0]
    interior_live = (lax.iota(jnp.int32, interior) < live_count)[:, None]
    masked = jnp.where(interior_live, own_coupling, 0.0)
    own_tiles = lax.dynamic_index_in_dim(iface_tiles, self_index, 0, keepdims=False)
    row_order = jnp.argsort(own_tiles % rows_grid, stable=True)
    col_order = jnp.argsort(own_tiles % cols_grid, stable=True)
    weighted = jnp.dot(
        own_factor, masked, precision=lax.Precision.HIGHEST, preferred_element_type=jnp.float32
    )
    weighted = jnp.where(interior_live, weighted, 0.0).reshape(interior, tile_count, tile_width)
    row_part = jnp.take(weighted, row_order, axis=1).reshape(
        interior, rows_grid, rows_per, tile_width
    )
    col_part = jnp.take(weighted, col_order, axis=1).reshape(
        interior, cols_grid, cols_per, tile_width
    )
    contribution = -jnp.einsum(
        "kprt,kqcu->pqrctu", row_part, col_part, precision=lax.Precision.HIGHEST
    )
    received = lax.all_to_all(
        contribution.reshape(rows_grid * cols_grid, rows_per, cols_per, tile_width, tile_width),
        ("prow", "pcol"),
        split_axis=0,
        concat_axis=0,
        tiled=True,
    )
    sorted_rows = jnp.take_along_axis(
        iface_tiles, jnp.argsort(iface_tiles % rows_grid, axis=1, stable=True), axis=1
    )
    sorted_rows = sorted_rows.reshape(domains, rows_grid, rows_per)
    sorted_cols = jnp.take_along_axis(
        iface_tiles, jnp.argsort(iface_tiles % cols_grid, axis=1, stable=True), axis=1
    )
    sorted_cols = sorted_cols.reshape(domains, cols_grid, cols_per)
    target_rows = lax.dynamic_index_in_dim(sorted_rows, prow_index, 1, keepdims=False) // rows_grid
    target_cols = lax.dynamic_index_in_dim(sorted_cols, pcol_index, 1, keepdims=False) // cols_grid
    slot_ids = (target_rows[:, :, None] * local_cols + target_cols[:, None, :]).reshape(-1)
    base_tiles = interface_block.reshape(local_rows * local_cols, tile_width, tile_width)
    summed = base_tiles.at[slot_ids].add(received.reshape(-1, tile_width, tile_width))
    schur = summed.reshape(interface_block.shape)
    column = summed.reshape(local_rows, local_cols, tile_width, tile_width)[:, 0]
    diag_block = broadcast(column[0], "prow", 0)
    factored = solve_panel(diag_block, column)
    panel = broadcast(factored, "pcol", 0)
    own_share = lax.dynamic_slice_in_dim(panel, pcol_index * share_rows, share_rows, 1)
    return (schur, own_share[None])


def solution(mesh):
    in_specs = (
        P(),
        P(("prow", "pcol")),
        P(("prow", "pcol"), None, None),
        P(("prow", "pcol"), None, None),
        P("prow", None, "pcol", None, None, None),
    )
    out_specs = (P("prow", None, "pcol", None, None, None), P("prow", None, "pcol", None))
    return jax.shard_map(shards, mesh=mesh, in_specs=in_specs, out_specs=out_specs, check_vma=False)
```

profile of v0, /device:TPU:0, one launch (start us, length us, event | category | flops | bytes accessed | tf_op | source)
XLA Modules:
  0.0 673.4 jit_solution(10466884502546801936)
XLA Ops:
  7.2 8.0 %copy.40 = f32[1,8,1,16,128,128]{5,4,3,2,1,0:T(8,128)} copy(f32[1,8,1,16,128,128]{5,4,3,2,1,0:T(8,128)} %param.13) | data formatting | bytes 16777216
  15.2 0.2 dynamic-slice_reduce_fusion
  15.4 1.2 sort.64
  16.6 1.2 sort.65
  18.6 16.4 %fusion.3 = f32[2048,512]{1,0:T(8,128)} fusion(f32[1,512,2048]{2,1,0:T(8,128)} %param.11, pred[512]{0:T(512)(128)(4,1)S(1)} %iota_compare_fusion.2, f32[1,512,512]{2,1,0:T(8,128)S(1)} %copy-done), kind=kOutput, calls=%fused_computation.9 | convolution fusion | flops 6444548096 | bytes 9437696 | tf_op jit(solution)/shard_map/dot_general | solution.py:42
  35.0 5.0 gather_fusion.2
  40.0 5.0 gather_fusion.3
  44.9 2.9 broadcast_select_fusion.1
  47.9 0.5 copy-done.3
  48.4 0.6 broadcast_select_fusion
  49.0 30.0 %negate_bitcast_fusion = f32[8,4,2,4,128,128]{4,5,2,0,3,1:T(8,128)} fusion(f32[512,4,4,128,1,1]{0,3,5,4,2,1:T(8,128)S(1)} %bitcast.89, f32[512,8,2,128,1,1]{0,3,2,1,5,4:T(8,128)S(1)} %bitcast.90), kind=kOutput, calls=%fused_computation.5 | convolution fusion | flops 25773998080 | bytes 25165824 | tf_op jit(solution)/shard_map/kprt,kqcu->pqrctu/dot_general | solution.py:52
  79.0 17.4 %copy.23 = f32[8,4,2,4,128,128]{5,4,3,2,1,0:T(8,128)} copy(f32[8,4,2,4,128,128]{4,5,2,0,3,1:T(8,128)} %negate_bitcast_fusion) | data formatting | bytes 33554432 | tf_op jit(solution)/shard_map/neg | solution.py:52
  96.4 7.5 %all-to-all-start = ((f32[32,2,4,128,128]{4,3,2,1,0:T(8,128)}), f32[32,2,4,128,128]{4,3,2,1,0:T(8,128)}, u32[]{:S(2)}, u32[]{:S(2)}) async-start(f32[32,2,4,128,128]{4,3,2,1,0:T(8,128)} %bitcast.86), calls=%async_computation | async-start | bytes 33554432 | tf_op jit(solution)/shard_map/all_to_all | solution.py:55
  103.9 0.7 sort.63
  104.8 3.9 gather_fusion.1
  109.0 0.7 sort.62
  109.9 3.9 gather_fusion
  114.3 362.2 %all-to-all-done = f32[32,2,4,128,128]{4,3,2,1,0:T(8,128)} async-done(((f32[32,2,4,128,128]{4,3,2,1,0:T(8,128)}), f32[32,2,4,128,128]{4,3,2,1,0:T(8,128)}, u32[]{:S(2)}, u32[]{:S(2)}) %all-to-all-start) | async-done | bytes 16777248 | tf_op jit(solution)/shard_map/all_to_all | solution.py:55
  476.4 51.4 %scatter_fusion = f32[128,128,128]{2,1,0:T(8,128)} fusion(f32[128,128,128]{2,1,0:T(8,128)} %bitcast.84, s32[256]{0:T(256)S(1)} %bitcast.95, f32[256,128,128]{2,1,0:T(8,128)} %bitcast.24), kind=kCustom, calls=%fused_computation.4 | custom fusion | flops 4194304 | bytes 50332672 | tf_op jit(solution)/shard_map/scatter-add | solution.py:74
  527.9 9.1 %copy.24 = f32[128,128,128]{1,2,0:T(8,128)} copy(f32[128,128,128]{2,1,0:T(8,128)} %scatter_fusion) | data formatting | bytes 16777216 | tf_op jit(solution)/shard_map/scatter-add | solution.py:74
  536.9 1.5 fusion.10
  538.4 0.3 all-reduce.5.cloned.1.call-start
  538.7 65.0 %all-reduce.3.cloned.1.call-done = f32[128,128]{0,1:T(8,128)} async-done(((f32[128,128]{0,1:T(8,128)}), f32[128,128]{0,1:T(8,128)}) %all-reduce.3.cloned.1.call-update) | async-done | bytes 65552 | tf_op jit(solution)/shard_map/psum | solution.py:9
  603.7 0.9 copy.25
  604.7 0.9 fusion.13
  605.6 11.7 %cholesky.15 = f32[128,128]{1,0:T(8,128)S(1)} custom-call(f32[128,128]{1,0:T(8,128)S(1)} %fusion.12), custom_call_target="Cholesky" | custom-call | tf_op jit(solution)/shard_map/jit(cholesky)/cholesky | solution.py:13
  617.4 0.6 compare_reduce_fusion
  618.0 0.7 fusion.9
  618.7 9.8 %custom-call.7 = f32[1,128,128]{1,2,0:T(8,128)S(1)} custom-call(f32[1,128,128]{2,1,0:T(8,128)S(1)} %fusion.9), custom_call_target="InvertDiagBlocksLowerTriangular" | custom-call | tf_op jit(solution)/shard_map/jit(_solve_triangular)/triangular_solve | solution.py:15
  628.5 2.9 convolution_select_fusion
  631.4 33.5 %all-reduce.5.cloned.1.call-done = f32[8,128,128]{2,1,0:T(8,128)} async-done(((f32[8,128,128]{2,1,0:T(8,128)}), f32[8,128,128]{2,1,0:T(8,128)}) %all-reduce.5.cloned.1.call-update) | async-done | bytes 524304 | tf_op jit(solution)/shard_map/psum | solution.py:9
  664.9 1.6 dynamic-slice_bitcast_fusion
  (43 shorter events, 1.4 us)
Async XLA Ops:
  7.2 11.4 %copy-start = (f32[1,512,512]{2,1,0:T(8,128)S(1)}, f32[1,512,512]{2,1,0:T(8,128)}, u32[]{:S(2)}) copy-start(f32[1,512,512]{2,1,0:T(8,128)} %param.12) | copy-start | bytes 3145732
  7.2 8.0 %copy-start.2 = (s32[32,16]{0,1:T(8,128)S(1)}, s32[32,16]{0,1:T(8,128)}, u32[]{:S(2)}) copy-start(s32[32,16]{0,1:T(8,128)} %param.9) | copy-start | bytes 6148
  44.9 3.4 copy-start.3
  96.4 380.1 %all-to-all-start = ((f32[32,2,4,128,128]{4,3,2,1,0:T(8,128)}), f32[32,2,4,128,128]{4,3,2,1,0:T(8,128)}, u32[]{:S(2)}, u32[]{:S(2)}) async-start(f32[32,2,4,128,128]{4,3,2,1,0:T(8,128)} %bitcast.86), calls=%async_computation | async-start | bytes 33554432 | tf_op jit(solution)/shard_map/all_to_all | solution.py:55
  103.9 499.9 %all-reduce.3.cloned.1.call-start = ((), (), s32[]{:S(2)}) async-start(), calls=%async_computation.1 | async-start | bytes 131072 | tf_op jit(solution)/shard_map/psum | solution.py:9
  527.9 138.7 %copy-start.1 = (f32[1,512,512]{2,1,0:T(8,128)S(1)}, f32[1,512,512]{2,1,0:T(8,128)}, u32[]{:S(2)}) copy-start(f32[1,512,512]{2,1,0:T(8,128)} %param.12) | copy-start | bytes 3145732
  538.4 126.5 %all-reduce.5.cloned.1.call-start = ((), (), s32[]{:S(2)}) async-start(), calls=%async_computation.2 | async-start | bytes 1048576 | tf_op jit(solution)/shard_map/psum | solution.py:9
Sparse Core Ops, SparseCore 0:
  538.6 65.1 all-reduce.2
  631.6 33.3 all-reduce.4
where the time goes:
time: 675 us; the launch traced here: 673 us
  waiting for transfers between devices  461 us (68%)
  other arithmetic  84.2 us (12%)
  local copies, waits for them, and re-layouts  56.4 us (8%)
  matrix products  49.3 us (7%)
  between operations  14.9 us (2%)
  starting transfers between devices  7.76 us (1%)
    all_to_all x1, waiting for transfers between devices, shards(): lax.all_to_all(contribution.reshape(rows_grid * cols_grid, rows_per, cols...  362 us
    psum x2, waiting for transfers between devices, broadcast(): return lax.psum(block, axis)  98.5 us
    scatter-add x1, other arithmetic, shards(): base_tiles.at[slot_ids].add(received.reshape(-1, tile_width, tile_width))  51.4 us
    dot_general x1, matrix products, shards(): jnp.einsum('kprt,kqcu->pqrctu', row_part, col_part, precision=lax.Precisi...  30 us
    neg x1, local copies, waits for them, and re-layouts, shards(): -jnp.einsum('kprt,kqcu->pqrctu', row_part, col_part, precision=lax.Precis...  17.4 us
    dot_general x1, matrix products, shards(): jnp.dot(own_factor, masked, precision=lax.Precision.HIGHEST, preferred_el...  16.4 us
  transfers between devices with their start and end apart: 3, of which 3 were waited for; matrix products, arithmetic and copies ran while one was open for 2% of the time, Pallas kernels for 0%

commit v1 on v0

v1 whole, which is shorter than its diff:
```python
import functools

import jax
import jax.numpy as jnp
from jax import lax
from jax.experimental import pallas as pl
from jax.experimental.pallas import tpu as pltpu
from jax.sharding import Mesh, PartitionSpec as P

HIGHEST = lax.Precision.HIGHEST


def split(x):
    high = x.astype(jnp.bfloat16)
    low = (x - high.astype(jnp.float32)).astype(jnp.bfloat16)
    return high, low


def dot3(a_high, a_low, b_high, b_low):
    dot = functools.partial(jnp.dot, preferred_element_type=jnp.float32)
    return dot(a_high, b_high) + (dot(a_high, b_low) + dot(a_low, b_high))


def weigh_kernel(info, factor_ref, left_ref, right_ref, out_ref, high_ref, low_ref):
    @pl.when(pl.program_id(0) == 0)
    def _():
        high, low = split(factor_ref[...])
        high_ref[...] = high
        low_ref[...] = low

    block = jnp.concatenate([left_ref[...], right_ref[...]], axis=1)
    live = lax.broadcasted_iota(jnp.int32, block.shape, 0) < info[0]
    high, low = split(jnp.where(live, block, 0.0))
    product = dot3(high_ref[...], low_ref[...], high, low)
    out_ref[...] = jnp.where(live, product, 0.0)


def weigh(info, factor, coupling, width):
    interior, iface = coupling.shape
    pairs = iface // width // 2
    return pl.pallas_call(
        weigh_kernel,
        grid_spec=pltpu.PrefetchScalarGridSpec(
            num_scalar_prefetch=1,
            grid=(pairs,),
            in_specs=[
                pl.BlockSpec((interior, interior), lambda i, info: (0, 0)),
                pl.BlockSpec((interior, width), lambda i, info: (0, info[1 + 2 * i])),
                pl.BlockSpec((interior, width), lambda i, info: (0, info[2 + 2 * i])),
            ],
            out_specs=pl.BlockSpec((interior, 2 * width), lambda i, info: (0, i)),
            scratch_shapes=[pltpu.VMEM((interior, interior), jnp.bfloat16)] * 2,
        ),
        out_shape=jax.ShapeDtypeStruct((interior, iface), jnp.float32),
        compiler_params=pltpu.CompilerParams(vmem_limit_bytes=24 << 20),
        cost_estimate=pl.CostEstimate(
            flops=6 * interior * interior * iface, bytes_accessed=8 * interior * iface, transcendentals=0
        ),
        name="weigh",
    )(info, factor, coupling, coupling)


def gram_kernel(rows_grid, cols_grid, width, half_ref, w_ref, out_ref, high_ref, low_ref):
    step = pl.program_id(0)
    iface = w_ref.shape[1]
    block = iface // rows_grid
    rows_per = block // width

    @pl.when(step == 0)
    def _():
        for m in range(rows_grid):
            high, low = split(w_ref[:, m * block : (m + 1) * block])
            high_ref[:, m * block : (m + 1) * block] = high
            low_ref[:, m * block : (m + 1) * block] = low

    own = half_ref[0] * (rows_grid // 2) + step
    rows = w_ref[:, pl.ds(pl.multiple_of(own * block, block), block)]
    row_high, row_low = split(rows.T)
    for m in range(rows_grid):
        q, lap = m % cols_grid, m // cols_grid
        cols = slice(m * block, (m + 1) * block)
        product = dot3(row_high, row_low, high_ref[:, cols], low_ref[:, cols])
        for r in range(rows_per):
            for c in range(rows_per):
                out_ref[q, r, lap * rows_per + c] = product[
                    r * width : (r + 1) * width, c * width : (c + 1) * width
                ]


def gram(half, weighted, rows_grid, cols_grid, width):
    interior, iface = weighted.shape
    rows_per = iface // width // rows_grid
    cols_per = iface // width // cols_grid
    steps = rows_grid // 2
    return pl.pallas_call(
        functools.partial(gram_kernel, rows_grid, cols_grid, width),
        grid_spec=pltpu.PrefetchScalarGridSpec(
            num_scalar_prefetch=1,
            grid=(steps,),
            in_specs=[pl.BlockSpec((interior, iface), lambda i, half: (0, 0))],
            out_specs=pl.BlockSpec(
                (cols_grid, rows_per, cols_per, width, width), lambda i, half: (i, 0, 0, 0, 0)
            ),
            scratch_shapes=[pltpu.VMEM((interior, iface), jnp.bfloat16)] * 2,
        ),
        out_shape=jax.ShapeDtypeStruct(
            (steps * cols_grid, rows_per, cols_per, width, width), jnp.float32
        ),
        compiler_params=pltpu.CompilerParams(vmem_limit_bytes=32 << 20),
        cost_estimate=pl.CostEstimate(
            flops=3 * interior * iface * iface, bytes_accessed=4 * interior * iface + 2 * iface * iface, transcendentals=0
        ),
        name="gram",
    )(half, weighted)


def subtract_kernel(slots, base_ref, parts_ref, out_ref):
    step = pl.program_id(0)

    @pl.when(step == 0)
    def _():
        def take(i, carry):
            out_ref[i] = base_ref[i]
            return carry

        lax.fori_loop(0, base_ref.shape[0], take, 0)

    count = parts_ref.shape[1]
    for i in range(count):
        slot = slots[step * count + i]
        out_ref[slot] = out_ref[slot] - parts_ref[0, i]


def subtract(slots, base, parts):
    tiles, width = base.shape[0], base.shape[-1]
    senders, count = parts.shape[:2]
    return pl.pallas_call(
        subtract_kernel,
        grid_spec=pltpu.PrefetchScalarGridSpec(
            num_scalar_prefetch=1,
            grid=(senders,),
            in_specs=[
                pl.BlockSpec((tiles, width, width), lambda i, slots: (0, 0, 0)),
                pl.BlockSpec((1, count, width, width), lambda i, slots: (i, 0, 0, 0)),
            ],
            out_specs=pl.BlockSpec((tiles, width, width), lambda i, slots: (0, 0, 0)),
        ),
        out_shape=jax.ShapeDtypeStruct(base.shape, jnp.float32),
        compiler_params=pltpu.CompilerParams(vmem_limit_bytes=44 << 20),
        cost_estimate=pl.CostEstimate(
            flops=parts.size, bytes_accessed=4 * parts.size + 8 * base.size, transcendentals=0
        ),
        name="subtract",
    )(slots, base, parts)


def shards(iface_tiles, interior_sizes, coupling, factor_inverse, interface_block):
    halves = lax.axis_size("half")
    half_rows = lax.axis_size("sub")
    cols_grid = lax.axis_size("pcol")
    rows_grid = halves * half_rows
    half = lax.axis_index("half")
    prow_index = half * half_rows + lax.axis_index("sub")
    pcol_index = lax.axis_index("pcol")
    self_index = prow_index * cols_grid + pcol_index
    domains, tile_count = iface_tiles.shape
    width = interface_block.shape[-1]
    local_rows, local_cols = interface_block.shape[1], interface_block.shape[3]
    rows_per = tile_count // rows_grid
    cols_per = tile_count // cols_grid
    laps = rows_grid // cols_grid
    share = width // cols_grid
    devices = rows_grid * cols_grid

    order = jnp.argsort(iface_tiles % rows_grid, axis=1, stable=True)
    sorted_tiles = jnp.take_along_axis(iface_tiles, order, axis=1)
    own_order = lax.dynamic_index_in_dim(order, self_index, 0, keepdims=False)
    own_sorted = lax.dynamic_index_in_dim(sorted_tiles, self_index, 0, keepdims=False)
    info = jnp.concatenate([interior_sizes, own_order.astype(jnp.int32)])
    half_info = half.astype(jnp.int32).reshape(1)

    weighted = weigh(info, factor_inverse[0], coupling[0], width)
    across = lax.ppermute(weighted, "half", [(h, (h + 1) % halves) for h in range(halves)])

    own_part = gram(half_info, weighted, rows_grid, cols_grid, width)
    own_received = lax.all_to_all(own_part, ("sub", "pcol"), split_axis=0, concat_axis=0, tiled=True)

    base = interface_block.reshape(local_rows * local_cols, width, width)
    zero_tile = sum(
        jnp.where(own_sorted[r] == 0, weighted[:, r * width : (r + 1) * width], 0.0)
        for r in range(rows_per)
    )
    diag = jnp.where(self_index == 0, base[0], 0.0) - jnp.einsum(
        "kt,ku->tu", zero_tile, zero_tile, precision=HIGHEST
    )
    stride = 1
    while stride < devices:
        axes = ("half", "sub", "pcol")
        diag = diag + lax.ppermute(diag, axes, [(d, d ^ stride) for d in range(devices)])
        stride *= 2
    lower = jnp.linalg.cholesky(0.5 * (diag + diag.T))
    inverse = jax.scipy.linalg.solve_triangular(lower, jnp.eye(width, dtype=jnp.float32), lower=True)

    far_part = gram(half_info, across, rows_grid, cols_grid, width)
    far_received = lax.all_to_all(far_part, ("sub", "pcol"), split_axis=0, concat_axis=0, tiled=True)

    by_row = sorted_tiles.reshape(domains, rows_grid, rows_per)
    target_rows = lax.dynamic_index_in_dim(by_row, prow_index, 1, keepdims=False) // rows_grid
    by_col = sorted_tiles.reshape(domains, laps, cols_grid, rows_per)
    target_cols = lax.dynamic_index_in_dim(by_col, pcol_index, 2, keepdims=False)
    target_cols = target_cols.reshape(domains, cols_per) // cols_grid
    slots = target_rows[:, :, None] * local_cols + target_cols[:, None, :]
    slots = slots.reshape(halves, -1)
    own_slots = lax.dynamic_index_in_dim(slots, half, 0, keepdims=False)
    far_slots = lax.dynamic_index_in_dim(slots, (half + 1) % halves, 0, keepdims=False)

    group = half_rows * cols_grid
    own_received = own_received.reshape(group, rows_per * cols_per, width, width)
    far_received = far_received.reshape(group, rows_per * cols_per, width, width)
    partial = subtract(own_slots, base, own_received)
    summed = subtract(far_slots, partial, far_received)
    schur = summed.reshape(interface_block.shape)

    column = summed.reshape(local_rows, local_cols, width, width)[:, 0]
    kept = jnp.where(pcol_index == 0, column[:, :share], 0.0)
    for q in range(1, cols_grid):
        kept = kept + lax.ppermute(column[:, q * share : (q + 1) * share], "pcol", [(0, q)])
    panel = jnp.einsum("atu,vu->atv", kept, inverse, precision=HIGHEST)
    return (schur, panel[None])


def solution(mesh):
    rows_grid, cols_grid = mesh.shape["prow"], mesh.shape["pcol"]
    grid = Mesh(
        mesh.devices.reshape(2, rows_grid // 2, cols_grid), ("half", "sub", "pcol")
    )
    prow = ("half", "sub")
    every = ("half", "sub", "pcol")
    in_specs = (
        P(),
        P(every),
        P(every, None, None),
        P(every, None, None),
        P(prow, None, "pcol", None, None, None),
    )
    out_specs = (P(prow, None, "pcol", None, None, None), P(prow, None, "pcol", None))
    return jax.shard_map(shards, mesh=grid, in_specs=in_specs, out_specs=out_specs, check_vma=False)
```

time: 675 us -> 482 us (0.71)
  waiting for transfers between devices: 461 us -> 320 us
  other arithmetic: 84.2 us -> 24.6 us
  Pallas kernels: 0 us -> 50.4 us
  matrix products: 49.3 us -> 3.03 us
  starting transfers between devices: 7.76 us -> 36.4 us
  local copies, waits for them, and re-layouts: 56.4 us -> 43.4 us
  between operations: 14.9 us -> 2.9 us
    all_to_all x1 -> x2, waiting for transfers between devices: 362 us -> 0.01 us  [the longest x1 0.01 us: shards(): lax.all_to_all(far_part, ('sub', 'pcol'), split_axis=0, concat_axis=0, ti...]
    ppermute x0 -> x9, waiting for transfers between devices: none -> 320 us  [the longest x1 216 us: shards(): lax.ppermute(weighted, 'half', [(h, (h + 1) % halves) for h in range(halv...]
    psum x2 -> x0, waiting for transfers between devices: 98.5 us -> none  [broadcast(): return lax.psum(block, axis)]
    scatter-add x1 -> x0, other arithmetic: 51.4 us -> none  [shards(): base_tiles.at[slot_ids].add(received.reshape(-1, tile_width, tile_width))]
    pallas_call x0 -> x5, Pallas kernels: none -> 50.4 us  [the longest x2 27.1 us: subtract(): pl.pallas_call(subtract_kernel, grid_spec=pltpu.PrefetchScalarGridSpec(nu...]
    dot_general x2, matrix products: 46.4 us -> 2.78 us  [the longest x1 1.84 us: shards(): jnp.einsum('kt,ku->tu', zero_tile, zero_tile, precision=HIGHEST)]
    ppermute x0 -> x9, starting transfers between devices: none -> 23.9 us  [the longest x3 14.8 us: shards(): lax.ppermute(column[:, q * share:(q + 1) * share], 'pcol', [(0, q)])]
    unnamed x9 -> x17, local copies, waits for them, and re-layouts: 8.51 us -> 27.9 us
  transfers between devices with their start and end apart: 3 -> 11, of which waited for: 3 -> 5; matrix products, arithmetic and copies ran while one was open for 2% -> 10% of each run, Pallas kernels for 0% -> 4%
where the time goes in v1:
time: 482 us; the launch traced here: 481 us
  waiting for transfers between devices  320 us (66%)
  Pallas kernels  50.4 us (10%)
  local copies, waits for them, and re-layouts  43.4 us (9%)
  starting transfers between devices  36.4 us (8%)
  other arithmetic  24.6 us (5%)
    ppermute x1, waiting for transfers between devices, shards(): lax.ppermute(weighted, 'half', [(h, (h + 1) % halves) for h in range(halv...  216 us
    ppermute x5, waiting for transfers between devices, shards(): lax.ppermute(diag, axes, [(d, d ^ stride) for d in range(devices)])  104 us
    unnamed x17, local copies, waits for them, and re-layouts  27.9 us
    pallas_call x2, Pallas kernels, subtract(): pl.pallas_call(subtract_kernel, grid_spec=pltpu.PrefetchScalarGridSpec(nu...  27.1 us
    pallas_call x2, Pallas kernels, gram(): pl.pallas_call(functools.partial(gram_kernel, rows_grid, cols_grid, width...  16.6 us
    ppermute x3, starting transfers between devices, shards(): lax.ppermute(column[:, q * share:(q + 1) * share], 'pcol', [(0, q)])  14.8 us
    another operation x3, other arithmetic, shards(): lower = jnp.linalg.cholesky(0.5 * (diag + diag.T))  12.4 us
    another operation x2, other arithmetic, shards(): jax.scipy.linalg.solve_triangular(lower, jnp.eye(width, dtype=jnp.float32...  10.5 us
  transfers between devices with their start and end apart: 11, of which 5 were waited for; matrix products, arithmetic and copies ran while one was open for 10% of the time, Pallas kernels for 4%

profile of v1, /device:TPU:0, one launch (start us, length us, event | category | flops | bytes accessed | tf_op | source)
XLA Modules:
  0.0 480.6 jit_solution(14778719527036894648)
XLA Ops:
  3.0 2.2 copy-done.2
  5.2 1.2 copy-done.6
  6.4 6.8 %weigh.1.w_ref = f32[512,2048]{1,0:T(8,128)S(1)} custom-call(s32[17]{0:T(128)S(1)} %pad_add_fusion.info, f32[512,512]{1,0:T(8,128)S(1)} %bitcast.59, f32[512,2048]{1,0:T(8,128)S(1)} %bitcast.57, f32[512,2048]{1,0:T(8,128)S(1)} %bitcast.58), custom_call_target="tpu_custom_call" | custom-call | flops 3221225472 | bytes 8388608 | tf_op jit(solution)/shard_map/weigh/pallas_call | solution.py:41
  13.2 8.3 %gram.2 = f32[16,2,4,128,128]{4,3,2,1,0:T(8,128)S(1)} custom-call(s32[1]{0:T(128)} %bitcast.8.half_ref, f32[512,2048]{1,0:T(8,128)S(1)} %weigh.1.w_ref), custom_call_target="tpu_custom_call" | custom-call | flops 6442450944 | bytes 12582912 | tf_op jit(solution)/shard_map/gram/pallas_call | solution.py:95
  21.5 3.4 copy-done.4
  24.9 2.0 copy-done.5
  26.8 6.4 %all-to-all-start = ((f32[16,2,4,128,128]{4,3,2,1,0:T(8,128)}), f32[16,2,4,128,128]{4,3,2,1,0:T(8,128)}, u32[]{:S(2)}, u32[]{:S(2)}) async-start(f32[16,2,4,128,128]{4,3,2,1,0:T(8,128)} %copy-done.4), calls=%async_computation | async-start | bytes 16777216 | tf_op jit(solution)/shard_map/all_to_all | solution.py:186
  33.2 2.7 collective-permute-start
  35.9 215.6 %collective-permute-done.w_ref = f32[512,2048]{1,0:T(8,128)S(1)} collective-permute-done((f32[512,2048]{1,0:T(8,128)}, f32[512,2048]{1,0:T(8,128)S(1)}, u32[]{:S(2)}, u32[]{:S(2)}) %collective-permute-start) | collective-permute-done | bytes 4194336 | tf_op jit(solution)/shard_map/ppermute | solution.py:183
  251.5 8.3 %gram.3 = f32[16,2,4,128,128]{4,3,2,1,0:T(8,128)S(1)} custom-call(s32[1]{0:T(128)} %bitcast.8.half_ref, f32[512,2048]{1,0:T(8,128)S(1)} %collective-permute-done.w_ref), custom_call_target="tpu_custom_call" | custom-call | flops 6442450944 | bytes 12582912 | tf_op jit(solution)/shard_map/gram/pallas_call | solution.py:95
  259.8 3.2 copy-done.3
  263.0 6.2 %all-to-all-start.1 = ((f32[16,2,4,128,128]{4,3,2,1,0:T(8,128)}), f32[16,2,4,128,128]{4,3,2,1,0:T(8,128)}, u32[]{:S(2)}, u32[]{:S(2)}) async-start(f32[16,2,4,128,128]{4,3,2,1,0:T(8,128)} %copy-done.3), calls=%async_computation.1 | async-start | bytes 16777216 | tf_op jit(solution)/shard_map/all_to_all | solution.py:205
  269.4 3.9 gather_fusion
  275.3 9.1 %copy.22 = f32[1,8,1,16,128,128]{4,5,3,1,2,0:T(8,128)} copy(f32[1,8,1,16,128,128]{5,4,3,2,1,0:T(8,128)} %param.9) | data formatting | bytes 16777216 | tf_op args[4]
  284.5 1.8 convolution_subtract_fusion
  287.6 1.9 collective-permute-start.5
  289.6 95.8 %collective-permute-done.5 = f32[128,128]{0,1:T(8,128)S(1)} collective-permute-done((f32[128,128]{0,1:T(8,128)S(1)}, f32[128,128]{0,1:T(8,128)S(1)}, u32[]{:S(2)}, u32[]{:S(2)}) %collective-permute-start.5) | collective-permute-done | bytes 65568 | tf_op jit(solution)/shard_map/ppermute | solution.py:199
  385.7 4.1 collective-permute-done.6
  390.8 9.0 %copy.23.base_ref = f32[128,128,128]{2,1,0:T(8,128)} copy(f32[128,128,128]{1,2,0:T(8,128)} %bitcast.61) | data formatting | bytes 16777216 | tf_op jit(solution)/shard_map/reshape | solution.py:188
  399.9 3.1 collective-permute-start.8
  403.1 3.4 collective-permute-done.8
  406.7 11.7 %cholesky.16 = f32[128,128]{1,0:T(8,128)S(1)} custom-call(f32[128,128]{1,0:T(8,128)S(1)} %fusion.12), custom_call_target="Cholesky" | custom-call | tf_op jit(solution)/shard_map/jit(cholesky)/cholesky | solution.py:201
  419.1 13.1 %subtract.2.base_ref = f32[128,128,128]{2,1,0:T(8,128)S(1)} custom-call(s32[128]{0:T(128)S(1)} %get-tuple-element.13.slots, f32[128,128,128]{2,1,0:T(8,128)} %copy.23.base_ref, f32[16,8,128,128]{3,2,1,0:T(8,128)} %bitcast.11.parts_ref), custom_call_target="tpu_custom_call" | custom-call | flops 2097152 | bytes 25165824 | tf_op jit(solution)/shard_map/subtract/pallas_call | solution.py:137
  432.2 3.4 copy-done
  435.6 3.4 copy-done.1
  439.0 14.0 %subtract.3 = f32[128,128,128]{2,1,0:T(8,128)} custom-call(s32[128]{0:T(128)S(1)} %get-tuple-element.14.slots, f32[128,128,128]{2,1,0:T(8,128)S(1)} %copy-done.1, f32[16,8,128,128]{3,2,1,0:T(8,128)} %bitcast.12.parts_ref), custom_call_target="tpu_custom_call" | custom-call | flops 2097152 | bytes 25165824 | tf_op jit(solution)/shard_map/subtract/pallas_call | solution.py:137
  452.9 1.1 slice_bitcast_fusion
  454.1 1.3 collective-permute-start.1
  455.4 12.2 %collective-permute-start.2 = (f32[8,32,128]{2,1,0:T(8,128)S(1)}, f32[8,32,128]{2,1,0:T(8,128)S(1)}, u32[]{:S(2)}, u32[]{:S(2)}) collective-permute-start(f32[8,32,128]{2,1,0:T(8,128)S(1)} %get-tuple-element.10), channel_id=1, source_target_pairs={{0,2},{4,6},{8,10},{12,14},{16,18},{20,22},{24,26},{28,30}} | collective-permute-start | bytes 393224 | tf_op jit(solution)/shard_map/ppermute | solution.py:227
  467.6 1.3 collective-permute-start.3
  469.5 9.8 %custom-call.7 = f32[1,128,128]{1,2,0:T(8,128)S(1)} custom-call(f32[1,128,128]{2,1,0:T(8,128)S(1)} %fusion.9), custom_call_target="InvertDiagBlocksLowerTriangular" | custom-call | tf_op jit(solution)/shard_map/jit(_solve_triangular)/triangular_solve | solution.py:202
  479.6 0.9 convolution_bitcast_fusion
  (53 shorter events, 7.2 us)
Async XLA Ops:
  3.0 2.2 copy-start.2
  5.2 1.2 copy-start.6
  21.5 3.4 copy-start.4
  24.9 2.0 copy-start.5
  26.8 236.1 %all-to-all-start = ((f32[16,2,4,128,128]{4,3,2,1,0:T(8,128)}), f32[16,2,4,128,128]{4,3,2,1,0:T(8,128)}, u32[]{:S(2)}, u32[]{:S(2)}) async-start(f32[16,2,4,128,128]{4,3,2,1,0:T(8,128)} %copy-done.4), calls=%async_computation | async-start | bytes 16777216 | tf_op jit(solution)/shard_map/all_to_all | solution.py:186
  33.2 218.3 %collective-permute-start = (f32[512,2048]{1,0:T(8,128)}, f32[512,2048]{1,0:T(8,128)S(1)}, u32[]{:S(2)}, u32[]{:S(2)}) collective-permute-start(f32[512,2048]{1,0:T(8,128)} %copy-done.5), channel_id=1, source_target_pairs={{0,16},{16,0},{1,17},{17,1},{2,18},{18,2},{3,19},{19,3},{4,20},{20... | collective-permute-start | bytes 12582920 | tf_op jit(solution)/shard_map/ppermute | solution.py:183
  259.8 3.2 copy-start.3
  263.0 6.4 %copy-start.7 = (s32[32,16]{0,1:T(8,128)S(1)}, s32[32,16]{0,1:T(8,128)}, u32[]{:S(2)}) copy-start(s32[32,16]{0,1:T(8,128)} %param.5) | copy-start | bytes 6148
  263.0 172.6 %all-to-all-start.1 = ((f32[16,2,4,128,128]{4,3,2,1,0:T(8,128)}), f32[16,2,4,128,128]{4,3,2,1,0:T(8,128)}, u32[]{:S(2)}, u32[]{:S(2)}) async-start(f32[16,2,4,128,128]{4,3,2,1,0:T(8,128)} %copy-done.3), calls=%async_computation.1 | async-start | bytes 16777216 | tf_op jit(solution)/shard_map/all_to_all | solution.py:205
  286.3 1.3 collective-permute-start.4
  287.6 97.8 %collective-permute-start.5 = (f32[128,128]{0,1:T(8,128)S(1)}, f32[128,128]{0,1:T(8,128)S(1)}, u32[]{:S(2)}, u32[]{:S(2)}) collective-permute-start(f32[128,128]{0,1:T(8,128)S(1)} %add.136), channel_id=1, source_target_pairs={{0,2},{1,3},{2,0},{3,1},{4,6},{5,7},{6,4},{7,5},{8,10},{9,11},{10,... | collective-permute-start | bytes 196616 | tf_op jit(solution)/shard_map/ppermute | solution.py:199
  385.4 4.3 collective-permute-start.6
  389.8 10.1 %collective-permute-start.7 = (f32[128,128]{0,1:T(8,128)S(1)}, f32[128,128]{0,1:T(8,128)S(1)}, u32[]{:S(2)}, u32[]{:S(2)}) collective-permute-start(f32[128,128]{0,1:T(8,128)S(1)} %add.138), channel_id=1, source_target_pairs={{0,8},{1,9},{2,10},{3,11},{4,12},{5,13},{6,14},{7,15},{8,0},{9,1},... | collective-permute-start | bytes 196616 | tf_op jit(solution)/shard_map/ppermute | solution.py:199
  399.9 6.5 %collective-permute-start.8 = (f32[128,128]{0,1:T(8,128)S(1)}, f32[128,128]{0,1:T(8,128)S(1)}, u32[]{:S(2)}, u32[]{:S(2)}) collective-permute-start(f32[128,128]{0,1:T(8,128)S(1)} %add.139), channel_id=1, source_target_pairs={{0,16},{1,17},{2,18},{3,19},{4,20},{5,21},{6,22},{7,23},{8,24},{9,... | collective-permute-start | bytes 196616 | tf_op jit(solution)/shard_map/ppermute | solution.py:199
  432.2 3.4 copy-start
  435.6 3.4 copy-start.1
  454.1 25.5 %collective-permute-start.1 = (f32[8,32,128]{2,1,0:T(8,128)S(1)}, f32[8,32,128]{2,1,0:T(8,128)S(1)}, u32[]{:S(2)}, u32[]{:S(2)}) collective-permute-start(f32[8,32,128]{2,1,0:T(8,128)S(1)} %get-tuple-element.8), channel_id=1, source_target_pairs={{0,1},{4,5},{8,9},{12,13},{16,17},{20,21},{24,25},{28,29}} | collective-permute-start | bytes 393224 | tf_op jit(solution)/shard_map/ppermute | solution.py:227
  455.4 24.2 %collective-permute-start.2 = (f32[8,32,128]{2,1,0:T(8,128)S(1)}, f32[8,32,128]{2,1,0:T(8,128)S(1)}, u32[]{:S(2)}, u32[]{:S(2)}) collective-permute-start(f32[8,32,128]{2,1,0:T(8,128)S(1)} %get-tuple-element.10), channel_id=1, source_target_pairs={{0,2},{4,6},{8,10},{12,14},{16,18},{20,22},{24,26},{28,30}} | collective-permute-start | bytes 393224 | tf_op jit(solution)/shard_map/ppermute | solution.py:227
  467.6 12.1 %collective-permute-start.3 = (f32[8,32,128]{2,1,0:T(8,128)S(1)}, f32[8,32,128]{2,1,0:T(8,128)S(1)}, u32[]{:S(2)}, u32[]{:S(2)}) collective-permute-start(f32[8,32,128]{2,1,0:T(8,128)S(1)} %get-tuple-element.9), channel_id=1, source_target_pairs={{0,3},{4,7},{8,11},{12,15},{16,19},{20,23},{24,27},{28,31}} | collective-permute-start | bytes 393224 | tf_op jit(solution)/shard_map/ppermute | solution.py:227

commit v2 on v1

--- a/solution.py
+++ b/solution.py
@@ -6,6 +6,7 @@
 from jax.experimental import pallas as pl
 from jax.experimental.pallas import tpu as pltpu
 from jax.sharding import Mesh, PartitionSpec as P
+
 
 HIGHEST = lax.Precision.HIGHEST
 
@@ -52,12 +53,44 @@
             scratch_shapes=[pltpu.VMEM((interior, interior), jnp.bfloat16)] * 2,
         ),
         out_shape=jax.ShapeDtypeStruct((interior, iface), jnp.float32),
-        compiler_params=pltpu.CompilerParams(vmem_limit_bytes=24 << 20),
+        compiler_params=pltpu.CompilerParams(vmem_limit_bytes=62 << 20),
         cost_estimate=pl.CostEstimate(
             flops=6 * interior * interior * iface, bytes_accessed=8 * interior * iface, transcendentals=0
         ),
         name="weigh",
     )(info, factor, coupling, coupling)
+
+
+def corner_kernel(info, factor_ref, column_ref, base_ref, out_ref):
+    block = column_ref[...]
+    live = (lax.broadcasted_iota(jnp.int32, block.shape, 0) < info[0]) & (info[2] == 1)
+    product = dot3(*split(factor_ref[...]), *split(jnp.where(live, block, 0.0)))
+    product = jnp.where(live, product, 0.0)
+    square = dot3(*split(product.T), *split(product))
+    out_ref[...] = jnp.where(info[3] == 1, base_ref[0], 0.0) - square
+
+
+def corner(info, factor, coupling, base):
+    interior, width = coupling.shape[0], base.shape[-1]
+    return pl.pallas_call(
+        corner_kernel,
+        grid_spec=pltpu.PrefetchScalarGridSpec(
+            num_scalar_prefetch=1,
+            grid=(1,),
+            in_specs=[
+                pl.BlockSpec((interior, interior), lambda i, info: (0, 0)),
+                pl.BlockSpec((interior, width), lambda i, info: (0, info[1])),
+                pl.BlockSpec((1, width, width), lambda i, info: (0, 0, 0)),
+            ],
+            out_specs=pl.BlockSpec((width, width), lambda i, info: (0, 0)),
+        ),
+        out_shape=jax.ShapeDtypeStruct((width, width), jnp.float32),
+        compiler_params=pltpu.CompilerParams(vmem_limit_bytes=62 << 20),
+        cost_estimate=pl.CostEstimate(
+            flops=6 * interior * interior * width, bytes_accessed=8 * interior * interior, transcendentals=0
+        ),
+        name="corner",
+    )(info, factor, coupling, base)
 
 
 def gram_kernel(rows_grid, cols_grid, width, half_ref, w_ref, out_ref, high_ref, low_ref):
@@ -106,7 +139,7 @@
         out_shape=jax.ShapeDtypeStruct(
             (steps * cols_grid, rows_per, cols_per, width, width), jnp.float32
         ),
-        compiler_params=pltpu.CompilerParams(vmem_limit_bytes=32 << 20),
+        compiler_params=pltpu.CompilerParams(vmem_limit_bytes=62 << 20),
         cost_estimate=pl.CostEstimate(
             flops=3 * interior * iface * iface, bytes_accessed=4 * interior * iface + 2 * iface * iface, transcendentals=0
         ),
@@ -146,7 +179,7 @@
             out_specs=pl.BlockSpec((tiles, width, width), lambda i, slots: (0, 0, 0)),
         ),
         out_shape=jax.ShapeDtypeStruct(base.shape, jnp.float32),
-        compiler_params=pltpu.CompilerParams(vmem_limit_bytes=44 << 20),
+        compiler_params=pltpu.CompilerParams(vmem_limit_bytes=62 << 20),
         cost_estimate=pl.CostEstimate(
             flops=parts.size, bytes_accessed=4 * parts.size + 8 * base.size, transcendentals=0
         ),
@@ -154,7 +187,7 @@
     )(slots, base, parts)
 
 
-def shards(iface_tiles, interior_sizes, coupling, factor_inverse, interface_block):
+def assemble(iface_tiles, interior_sizes, coupling, factor_inverse, interface_block):
     halves = lax.axis_size("half")
     half_rows = lax.axis_size("sub")
     cols_grid = lax.axis_size("pcol")
@@ -175,34 +208,8 @@
     order = jnp.argsort(iface_tiles % rows_grid, axis=1, stable=True)
     sorted_tiles = jnp.take_along_axis(iface_tiles, order, axis=1)
     own_order = lax.dynamic_index_in_dim(order, self_index, 0, keepdims=False)
-    own_sorted = lax.dynamic_index_in_dim(sorted_tiles, self_index, 0, keepdims=False)
     info = jnp.concatenate([interior_sizes, own_order.astype(jnp.int32)])
     half_info = half.astype(jnp.int32).reshape(1)
-
-    weighted = weigh(info, factor_inverse[0], coupling[0], width)
-    across = lax.ppermute(weighted, "half", [(h, (h + 1) % halves) for h in range(halves)])
-
-    own_part = gram(half_info, weighted, rows_grid, cols_grid, width)
-    own_received = lax.all_to_all(own_part, ("sub", "pcol"), split_axis=0, concat_axis=0, tiled=True)
-
-    base = interface_block.reshape(local_rows * local_cols, width, width)
-    zero_tile = sum(
-        jnp.where(own_sorted[r] == 0, weighted[:, r * width : (r + 1) * width], 0.0)
-        for r in range(rows_per)
-    )
-    diag = jnp.where(self_index == 0, base[0], 0.0) - jnp.einsum(
-        "kt,ku->tu", zero_tile, zero_tile, precision=HIGHEST
-    )
-    stride = 1
-    while stride < devices:
-        axes = ("half", "sub", "pcol")
-        diag = diag + lax.ppermute(diag, axes, [(d, d ^ stride) for d in range(devices)])
-        stride *= 2
-    lower = jnp.linalg.cholesky(0.5 * (diag + diag.T))
-    inverse = jax.scipy.linalg.solve_triangular(lower, jnp.eye(width, dtype=jnp.float32), lower=True)
-
-    far_part = gram(half_info, across, rows_grid, cols_grid, width)
-    far_received = lax.all_to_all(far_part, ("sub", "pcol"), split_axis=0, concat_axis=0, tiled=True)
 
     by_row = sorted_tiles.reshape(domains, rows_grid, rows_per)
     target_rows = lax.dynamic_index_in_dim(by_row, prow_index, 1, keepdims=False) // rows_grid
@@ -213,6 +220,41 @@
     slots = slots.reshape(halves, -1)
     own_slots = lax.dynamic_index_in_dim(slots, half, 0, keepdims=False)
     far_slots = lax.dynamic_index_in_dim(slots, (half + 1) % halves, 0, keepdims=False)
+
+    base = interface_block.reshape(local_rows * local_cols, width, width)
+    own_tiles = lax.dynamic_index_in_dim(iface_tiles, self_index, 0, keepdims=False)
+    corner_info = jnp.stack(
+        [
+            interior_sizes[0],
+            jnp.max(jnp.where(own_tiles == 0, lax.iota(jnp.int32, tile_count), 0)),
+            jnp.any(own_tiles == 0).astype(jnp.int32),
+            (self_index == 0).astype(jnp.int32),
+        ]
+    )
+    diag = corner(corner_info, factor_inverse[0], coupling[0], base)
+
+    def exchange(diag, strides):
+        for stride in strides:
+            pairs = [(d, d ^ stride) for d in range(devices)]
+            diag = diag + lax.ppermute(diag, ("half", "sub", "pcol"), pairs)
+        return diag
+
+    strides = [1 << k for k in range(devices.bit_length() - 1)]
+    near = half_rows * cols_grid // 4
+    diag = exchange(diag, [stride for stride in strides[::-1] if stride > near])
+    weighted = weigh(info, factor_inverse[0], coupling[0], width)
+    sent, diag = lax.optimization_barrier((weighted, diag))
+    across = lax.ppermute(sent, "half", [(h, (h + 1) % halves) for h in range(halves)])
+    diag = exchange(diag, [stride for stride in strides if stride <= near])
+    own_part = gram(half_info, weighted, rows_grid, cols_grid, width)
+    own_part, diag = lax.optimization_barrier((own_part, diag))
+    own_received = lax.all_to_all(own_part, ("sub", "pcol"), split_axis=0, concat_axis=0, tiled=True)
+    lower = jnp.linalg.cholesky(0.5 * (diag + diag.T))
+    inverse = jax.scipy.linalg.solve_triangular(lower, jnp.eye(width, dtype=jnp.float32), lower=True)
+    across, inverse, own_slots, far_slots = lax.optimization_barrier((across, inverse, own_slots, far_slots))
+
+    far_part = gram(half_info, across, rows_grid, cols_grid, width)
+    far_received = lax.all_to_all(far_part, ("sub", "pcol"), split_axis=0, concat_axis=0, tiled=True)
 
     group = half_rows * cols_grid
     own_received = own_received.reshape(group, rows_per * cols_per, width, width)
@@ -244,4 +286,4 @@
         P(prow, None, "pcol", None, None, None),
     )
     out_specs = (P(prow, None, "pcol", None, None, None), P(prow, None, "pcol", None))
-    return jax.shard_map(shards, mesh=grid, in_specs=in_specs, out_specs=out_specs, check_vma=False)
+    return jax.shard_map(assemble, mesh=grid, in_specs=in_specs, out_specs=out_specs, check_vma=False)

time: 482 us -> 446 us (0.925)
  local copies, waits for them, and re-layouts: 43.4 us -> 7.47 us
  Pallas kernels: 50.4 us -> 70.5 us
  waiting for transfers between devices: 320 us -> 307 us
  starting transfers between devices: 36.4 us -> 27.7 us
    ppermute x9, waiting for transfers between devices: 320 us -> 195 us  [the longest x1 186 us: assemble(): lax.ppermute(sent, 'half', [(h, (h + 1) % halves) for h in range(halves)])]
    all_to_all x2, waiting for transfers between devices: 0.01 us -> 112 us  [the longest x1 112 us: assemble(): lax.all_to_all(far_part, ('sub', 'pcol'), split_axis=0, concat_axis=0, ti...]
    unnamed x17 -> x2, local copies, waits for them, and re-layouts: 27.9 us -> 0.01 us
    reshape x1 -> x0, local copies, waits for them, and re-layouts: 8.98 us -> none  [shards(): base = interface_block.reshape(local_rows * local_cols, width, width)]
    ppermute x9, starting transfers between devices: 23.9 us -> 15.9 us  [the longest x5 7.98 us: exchange(): diag = diag + lax.ppermute(diag, ('half', 'sub', 'pcol'), pairs)]
    pallas_call x2, Pallas kernels: 16.6 us -> 23.7 us  [gram(): pl.pallas_call(functools.partial(gram_kernel, rows_grid, cols_grid, width...]
    pallas_call x2, Pallas kernels: 27.1 us -> 33.1 us  [subtract(): pl.pallas_call(subtract_kernel, grid_spec=pltpu.PrefetchScalarGridSpec(nu...]
    another operation x5 -> x6, other arithmetic: 22.9 us -> 24.1 us  [the longest x3 12.4 us: assemble(): lower = jnp.linalg.cholesky(0.5 * (diag + diag.T))]
  transfers between devices with their start and end apart: 11 -> 11, of which waited for: 5 -> 7; matrix products, arithmetic and copies ran while one was open for 10% -> 7% of each run, Pallas kernels for 4% -> 11%
where the time goes in v2:
time: 446 us; the launch traced here: 443 us
  waiting for transfers between devices  307 us (69%)
  Pallas kernels  70.5 us (16%)
  starting transfers between devices  27.7 us (6%)
  other arithmetic  27.6 us (6%)
  local copies, waits for them, and re-layouts  7.47 us (2%)
    ppermute x1, waiting for transfers between devices, assemble(): lax.ppermute(sent, 'half', [(h, (h + 1) % halves) for h in range(halves)])  186 us
    all_to_all x1, waiting for transfers between devices, assemble(): lax.all_to_all(far_part, ('sub', 'pcol'), split_axis=0, concat_axis=0, ti...  112 us
    pallas_call x2, Pallas kernels, subtract(): pl.pallas_call(subtract_kernel, grid_spec=pltpu.PrefetchScalarGridSpec(nu...  33.1 us
    pallas_call x2, Pallas kernels, gram(): pl.pallas_call(functools.partial(gram_kernel, rows_grid, cols_grid, width...  23.7 us
    another operation x3, other arithmetic, assemble(): lower = jnp.linalg.cholesky(0.5 * (diag + diag.T))  12.4 us
    another operation x2, other arithmetic, assemble(): jax.scipy.linalg.solve_triangular(lower, jnp.eye(width, dtype=jnp.float32...  10.4 us
    pallas_call x1, Pallas kernels, weigh(): pl.pallas_call(weigh_kernel, grid_spec=pltpu.PrefetchScalarGridSpec(num_s...  10.1 us
  transfers between devices with their start and end apart: 11, of which 7 were waited for; matrix products, arithmetic and copies ran while one was open for 7% of the time, Pallas kernels for 11%

profile of v2, /device:TPU:0, one launch (start us, length us, event | category | flops | bytes accessed | tf_op | source)
XLA Modules:
  0.0 443.3 jit_solution(13456470364846475113)
XLA Ops:
  1.3 1.4 fusion.20
  4.0 1.2 pad_add_fusion.1.info
  5.2 3.6 corner.1
  8.9 0.9 copy.17
  9.8 4.1 collective-permute-start
  13.9 0.7 sort.17
  15.4 2.2 collective-permute-done
  18.2 10.1 %weigh.1.w_ref = f32[512,2048]{1,0:T(8,128)} custom-call(s32[17]{0:T(128)} %pad_add_fusion.info, f32[512,512]{1,0:T(8,128)} %bitcast.62, f32[512,2048]{1,0:T(8,128)} %bitcast.55, f32[512,2048]{1,0:T(8,128)} %bitcast.56), custom_call_target="tpu_custom_call" | custom-call | flops 3221225472 | bytes 8388608 | tf_op jit(solution)/shard_map/weigh/pallas_call | solution.py:42
  28.4 1.2 collective-permute-done.3
  29.6 1.6 collective-permute-start.4
  31.2 2.8 collective-permute-done.4
  34.0 1.6 collective-permute-start.5
  35.6 11.8 %gram.2 = f32[16,2,4,128,128]{4,3,2,1,0:T(8,128)} custom-call(s32[1]{0:T(128)} %bitcast.6.half_ref, f32[512,2048]{1,0:T(8,128)} %weigh.1.w_ref), custom_call_target="tpu_custom_call" | custom-call | flops 6442450944 | bytes 12582912 | tf_op jit(solution)/shard_map/gram/pallas_call | solution.py:128
  47.4 4.9 %all-to-all-start = ((f32[16,2,4,128,128]{4,3,2,1,0:T(8,128)}), f32[16,2,4,128,128]{4,3,2,1,0:T(8,128)}, u32[]{:S(2)}, u32[]{:S(2)}) async-start(f32[16,2,4,128,128]{4,3,2,1,0:T(8,128)} %gram.2), calls=%async_computation | async-start | bytes 16777216 | tf_op jit(solution)/shard_map/all_to_all | solution.py:251
  52.4 3.4 collective-permute-start.2
  56.0 3.9 gather_fusion
  61.3 11.7 %cholesky.17 = f32[128,128]{1,0:T(8,128)S(1)} custom-call(f32[128,128]{1,0:T(8,128)S(1)} %fusion.8), custom_call_target="Cholesky" | custom-call | tf_op jit(solution)/shard_map/jit(cholesky)/cholesky | solution.py:252
  73.0 0.7 compare_reduce_fusion
  74.3 9.8 %custom-call.7 = f32[1,128,128]{1,2,0:T(8,128)S(1)} custom-call(f32[1,128,128]{2,1,0:T(8,128)S(1)} %fusion.4), custom_call_target="InvertDiagBlocksLowerTriangular" | custom-call | tf_op jit(solution)/shard_map/jit(_solve_triangular)/triangular_solve | solution.py:253
  84.4 186.0 %collective-permute-done.2.w_ref = f32[512,2048]{1,0:T(8,128)} collective-permute-done((f32[512,2048]{1,0:T(8,128)}, f32[512,2048]{1,0:T(8,128)}, u32[]{:S(2)}, u32[]{:S(2)}) %collective-permute-start.2) | collective-permute-done | bytes 4194336 | tf_op jit(solution)/shard_map/ppermute | solution.py:247
  270.4 11.9 %gram.3 = f32[16,2,4,128,128]{4,3,2,1,0:T(8,128)} custom-call(s32[1]{0:T(128)} %bitcast.6.half_ref, f32[512,2048]{1,0:T(8,128)} %collective-permute-done.2.w_ref), custom_call_target="tpu_custom_call" | custom-call | flops 6442450944 | bytes 12582912 | tf_op jit(solution)/shard_map/gram/pallas_call | solution.py:128
  282.3 6.9 %all-to-all-start.1 = ((f32[16,2,4,128,128]{4,3,2,1,0:T(8,128)}), f32[16,2,4,128,128]{4,3,2,1,0:T(8,128)}, u32[]{:S(2)}, u32[]{:S(2)}) async-start(f32[16,2,4,128,128]{4,3,2,1,0:T(8,128)} %gram.3), calls=%async_computation.1 | async-start | bytes 16777216 | tf_op jit(solution)/shard_map/all_to_all | solution.py:257
  289.2 16.4 %subtract.2.base_ref = f32[128,128,128]{2,1,0:T(8,128)} custom-call(s32[128]{0:T(128)} %get-tuple-element.16.slots, f32[128,128,128]{2,1,0:T(8,128)} %bitcast.58, f32[16,8,128,128]{3,2,1,0:T(8,128)} %bitcast.18.parts_ref), custom_call_target="tpu_custom_call" | custom-call | flops 2097152 | bytes 25165824 | tf_op jit(solution)/shard_map/subtract/pallas_call | solution.py:170
  305.6 111.9 %all-to-all-done.1 = f32[16,2,4,128,128]{4,3,2,1,0:T(8,128)} async-done(((f32[16,2,4,128,128]{4,3,2,1,0:T(8,128)}), f32[16,2,4,128,128]{4,3,2,1,0:T(8,128)}, u32[]{:S(2)}, u32[]{:S(2)}) %all-to-all-start.1) | async-done | bytes 8388640 | tf_op jit(solution)/shard_map/all_to_all | solution.py:257
  417.6 16.6 %subtract.3 = f32[128,128,128]{2,1,0:T(8,128)} custom-call(s32[128]{0:T(128)} %get-tuple-element.15.slots, f32[128,128,128]{2,1,0:T(8,128)} %subtract.2.base_ref, f32[16,8,128,128]{3,2,1,0:T(8,128)} %bitcast.19.parts_ref), custom_call_target="tpu_custom_call" | custom-call | flops 2097152 | bytes 25165824 | tf_op jit(solution)/shard_map/subtract/pallas_call | solution.py:170
  434.2 1.1 slice_bitcast_fusion
  435.3 1.8 collective-permute-start.6
  437.2 1.3 collective-permute-start.8
  438.5 1.3 collective-permute-start.7
  439.8 1.2 collective-permute-done.8
  441.0 1.4 collective-permute-done.7
  442.3 0.9 convolution_bitcast_fusion
  (40 shorter events, 4.6 us)
Async XLA Ops:
  0.6 13.3 %copy-start = (s32[32,16]{0,1:T(8,128)S(1)}, s32[32,16]{0,1:T(8,128)}, u32[]{:S(2)}) copy-start(s32[32,16]{0,1:T(8,128)} %param.5) | copy-start | bytes 6148
  9.8 7.8 %collective-permute-start = (f32[128,128]{0,1:T(8,128)S(1)}, f32[128,128]{0,1:T(8,128)S(1)}, u32[]{:S(2)}, u32[]{:S(2)}) collective-permute-start(f32[128,128]{0,1:T(8,128)S(1)} %copy.17), channel_id=1, source_target_pairs={{0,16},{1,17},{2,18},{3,19},{4,20},{5,21},{6,22},{7,23},{8,24},{9,... | collective-permute-start | bytes 196616 | tf_op jit(solution)/shard_map/ppermute | solution.py:239
  17.6 10.7 %collective-permute-start.1 = (f32[128,128]{0,1:T(8,128)S(1)}, f32[128,128]{0,1:T(8,128)S(1)}, u32[]{:S(2)}, u32[]{:S(2)}) collective-permute-start(f32[128,128]{0,1:T(8,128)S(1)} %add.117), channel_id=1, source_target_pairs={{0,8},{1,9},{2,10},{3,11},{4,12},{5,13},{6,14},{7,15},{8,0},{9,1},... | collective-permute-start | bytes 196616 | tf_op jit(solution)/shard_map/ppermute | solution.py:239
  28.3 1.3 collective-permute-start.3
  29.6 4.3 collective-permute-start.4
  34.0 13.4 %collective-permute-start.5 = (f32[128,128]{0,1:T(8,128)S(1)}, f32[128,128]{0,1:T(8,128)S(1)}, u32[]{:S(2)}, u32[]{:S(2)}) collective-permute-start(f32[128,128]{0,1:T(8,128)S(1)} %add.120), channel_id=1, source_target_pairs={{0,4},{1,5},{2,6},{3,7},{4,0},{5,1},{6,2},{7,3},{8,12},{9,13},{10,... | collective-permute-start | bytes 196616 | tf_op jit(solution)/shard_map/ppermute | solution.py:239
  47.4 234.9 %all-to-all-start = ((f32[16,2,4,128,128]{4,3,2,1,0:T(8,128)}), f32[16,2,4,128,128]{4,3,2,1,0:T(8,128)}, u32[]{:S(2)}, u32[]{:S(2)}) async-start(f32[16,2,4,128,128]{4,3,2,1,0:T(8,128)} %gram.2), calls=%async_computation | async-start | bytes 16777216 | tf_op jit(solution)/shard_map/all_to_all | solution.py:251
  52.4 218.1 %collective-permute-start.2 = (f32[512,2048]{1,0:T(8,128)}, f32[512,2048]{1,0:T(8,128)}, u32[]{:S(2)}, u32[]{:S(2)}) collective-permute-start(f32[512,2048]{1,0:T(8,128)} %weigh.1.w_ref), channel_id=1, source_target_pairs={{0,16},{16,0},{1,17},{17,1},{2,18},{18,2},{3,19},{19,3},{4,20},{20... | collective-permute-start | bytes 12582920 | tf_op jit(solution)/shard_map/ppermute | solution.py:247
  282.3 135.3 %all-to-all-start.1 = ((f32[16,2,4,128,128]{4,3,2,1,0:T(8,128)}), f32[16,2,4,128,128]{4,3,2,1,0:T(8,128)}, u32[]{:S(2)}, u32[]{:S(2)}) async-start(f32[16,2,4,128,128]{4,3,2,1,0:T(8,128)} %gram.3), calls=%async_computation.1 | async-start | bytes 16777216 | tf_op jit(solution)/shard_map/all_to_all | solution.py:257
  435.3 4.5 %collective-permute-start.6 = (f32[8,32,128]{2,1,0:T(8,128)S(1)}, f32[8,32,128]{2,1,0:T(8,128)S(1)}, u32[]{:S(2)}, u32[]{:S(2)}) collective-permute-start(f32[8,32,128]{2,1,0:T(8,128)S(1)} %get-tuple-element.26), channel_id=1, source_target_pairs={{0,1},{4,5},{8,9},{12,13},{16,17},{20,21},{24,25},{28,29}} | collective-permute-start | bytes 393224 | tf_op jit(solution)/shard_map/ppermute | solution.py:269
  437.2 3.8 collective-permute-start.8
  438.5 3.9 collective-permute-start.7
